TPU v7x, 32 devices: a whole 2x2x4 slice. The times are simulated.
32 devices in a mesh: gx: 4 (over y, core), gy: 2 (over x), gz: 4 (over z).
Axes of the slice: x: 2, y: 2, z: 4, core: 2. Of those that a mesh axis runs over, the one named last changes fastest.
Arguments:
- positions: float32 [3, 4, 2, 4, 4096], P(None, 'gx', 'gy', 'gz'), may hold values from 0 to 4, as said below
- velocities: float32 [3, 4, 2, 4, 4096], P(None, 'gx', 'gy', 'gz'), may hold values from -6 to 6
- strength: float32 [4, 2, 4, 4096], P('gx', 'gy', 'gz'), may hold values from 0.5 to 2
- charge: float32 [4, 2, 4, 4096], P('gx', 'gy', 'gz'), may hold values from -5 to 5
- bond_stiffness: float32 [2, 4, 2, 4, 4096], P(None, 'gx', 'gy', 'gz'), may hold values from 0.5 to 4
- bond_partner: int32 [2, 4, 2, 4, 4096], P(None, 'gx', 'gy', 'gz'), may hold values from 0 to 18431, as said below
- pair_blocks: int32 [4, 2, 4, 32, 8], P('gx', 'gy', 'gz'), may hold values from 0 to 143, as said below
- tile_count: int32 [4, 2, 4], P('gx', 'gy', 'gz'), may hold values from 1024 to 4096, as said below
- block_cell: int32 [4, 2, 4, 32], P('gx', 'gy', 'gz'), may hold values from 0 to 255
- cell_frac: float32 [3, 256], replicated, may hold values from 0 to 1
- bond_force: float32 [3, 4, 2, 4, 4096], P(None, 'gx', 'gy', 'gz'), may hold values from -6 to 6
- pair_force: float32 [3, 4, 2, 4, 4096], P(None, 'gx', 'gy', 'gz'), may hold values from -6 to 6
- far_force: float32 [3, 4, 2, 4, 4096], P(None, 'gx', 'gy', 'gz'), may hold values from -6 to 6
Outputs:
- positions_out: float32 [3, 4, 2, 4, 4096], P(None, 'gx', 'gy', 'gz')
- velocities_out: float32 [3, 4, 2, 4, 4096], P(None, 'gx', 'gy', 'gz')
Inputs may be any that keep to these rules, and one draw needn't show every extreme that they name: `positions`: each bead lies inside the unit cube of its block. `tile_count`: live beads of a tile fill its slots from 0 upward; some tile is full in every draw. `bond_partner`: A live bead's partners are live beads of its own block or of one of the six blocks sharing a face with it; an empty slot names its own column. `pair_blocks`: each row begins with the block itself and then lists distinct blocks that share a face, an edge or a corner with it.
All inputs are finite; a program needn't handle non-finite values.
Results may differ from a plain program's by a relative error of at most 0.0003.
Values sent between devices are 32-bit elements; how exact they have to be, the bound alone decides.
A program may use at most 64 MiB of HBM per device.

v0:
```python
import functools
import itertools
import math

import jax
import jax.numpy as jnp
from jax import lax
from jax.experimental import pallas as pl
from jax.experimental.pallas import tpu as pltpu
from jax.sharding import PartitionSpec as P

SBX = 4
SBY = 4
SBZ = 2
BLK = 128
NB = SBX * SBY * SBZ
AXES = ("gx", "gy", "gz")
SIDES = (SBX, SBY, SBZ)

inner_step = 0.1
outer_half = 2.0 * inner_step
half_step = 0.5 * inner_step
gauss_width = 0.25
cutoff_radius = 1.0
pair_scale = 0.1
soften = 1.0
coulomb = 0.02

MESH = pl.DeviceIdType.MESH
FACES = ((0, 0, 0), (-1, 0, 0), (1, 0, 0), (0, -1, 0), (0, 1, 0), (0, 0, -1), (0, 0, 1))
DIRS = sorted(
    (d for d in itertools.product((-1, 0, 1), repeat=3) if d != (0, 0, 0)),
    key=lambda d: (sum(abs(c) for c in d) != 1, -abs(d[2]), d),
)


def bf(x):
    return x.astype(jnp.bfloat16).astype(jnp.float32)


def split3(x):
    high = bf(x)
    middle = bf(x - high)
    return high, middle, x - high - middle


def kernel(
    sizes,
    pos_ref,
    vel_ref,
    str_ref,
    chg_ref,
    stiff_ref,
    part_ref,
    frac_ref,
    bf_ref,
    pf_ref,
    ff_ref,
    list_ref,
    count_ref,
    cell_ref,
    pos_out,
    vel_out,
    ext,
    v_s,
    spring,
    lane_s,
    face_s,
    own_s,
    far_s,
    val_s,
    hot,
    red_x,
    red_y,
    red_z,
    send_sem,
    recv_sem,
    rsend_sem,
    rrecv_sem,
):
    me = tuple(lax.axis_index(a) for a in AXES)
    cells = frac_ref.shape[1]
    f32 = jnp.float32

    def shifted(axis, step):
        ids = list(me)
        ids[axis] = lax.rem(me[axis] + step + sizes[axis], sizes[axis])
        return tuple(ids)

    def toward(d):
        return tuple(
            me[a] if d[a] == 0 else lax.rem(me[a] + d[a] + sizes[a], sizes[a]) for a in range(3)
        )

    barrier = pltpu.get_barrier_semaphore()
    expected = 0
    for d in DIRS:
        pl.semaphore_signal(barrier, inc=1, device_id=toward(d), device_id_type=MESH)
        expected += 1
    for axis in range(3):
        for step in range(2, sizes[axis] - 1):
            pl.semaphore_signal(barrier, inc=1, device_id=shifted(axis, step), device_id_type=MESH)
            expected += 1

    row4 = lax.broadcasted_iota(jnp.int32, (4, BLK), 0)
    row8 = lax.broadcasted_iota(jnp.int32, (8, BLK), 0)

    def vec4(a, b, c, last=0.0):
        return jnp.where(row4 == 0, a, jnp.where(row4 == 1, b, jnp.where(row4 == 2, c, last)))

    def vec8(a, b, c):
        r = row8 % 4
        return jnp.where(r == 0, a, jnp.where(r == 1, b, jnp.where(r == 2, c, 0.0)))

    coord = row4 < 3

    live = (
        lax.broadcasted_iota(jnp.int32, (NB, BLK), 0) * BLK
        + lax.broadcasted_iota(jnp.int32, (NB, BLK), 1)
        < count_ref[0, 0, 0]
    ).astype(f32)
    strength_live = str_ref[...] * live
    charge_live = chg_ref[...] * live

    def spots(body):
        def plane(bx, carry):
            for by in range(SBY):
                for bz in range(SBZ):
                    body(bx, by, bz, (bx * SBY + by) * SBZ + bz)
            return carry

        lax.fori_loop(0, SBX, plane, 0)

    for bx, by, bz in itertools.product(range(SBX), range(SBY), range(SBZ)):
        b = (bx * SBY + by) * SBZ + bz
        at = (bx, by, bz)
        for c in range(3):
            v = (
                vel_ref[c, b : b + 1, :]
                + outer_half * ff_ref[c, b : b + 1, :]
                + inner_step * pf_ref[c, b : b + 1, :]
                + half_step * bf_ref[c, b : b + 1, :]
            )
            v_s[b, c : c + 1, :] = v
            ext[0, bx + 1, by + 1, bz + 1, c : c + 1, :] = (
                pos_ref[c, b : b + 1, :] - float(at[c])
            ) + inner_step * v
        v_s[b, 3:4, :] = jnp.zeros((1, BLK), f32)
        ext[0, bx + 1, by + 1, bz + 1, 3:4, :] = strength_live[b : b + 1, :]

    pl.semaphore_wait(barrier, expected)

    def box(d, ghost):
        out = []
        for a in range(3):
            if d[a] == 0:
                out.append(pl.ds(1, SIDES[a]))
            elif ghost:
                out.append(pl.ds(0 if d[a] == 1 else SIDES[a] + 1, 1))
            else:
                out.append(pl.ds(SIDES[a] if d[a] == 1 else 1, 1))
        return tuple(out)

    def halo(n, k):
        d = DIRS[k]
        return pltpu.make_async_remote_copy(
            src_ref=ext.at[(n,) + box(d, False)],
            dst_ref=ext.at[(n,) + box(d, True)],
            send_sem=send_sem.at[n, k],
            recv_sem=recv_sem.at[n, k],
            device_id=toward(d),
            device_id_type=MESH,
        )

    reds = (red_x, red_y, red_z)
    base = (0, sizes[0], sizes[0] + sizes[1])

    def exchange(axis, step, slot):
        return pltpu.make_async_remote_copy(
            src_ref=reds[axis].at[slot],
            dst_ref=reds[axis].at[slot],
            send_sem=rsend_sem.at[base[axis] + step],
            recv_sem=rrecv_sem.at[base[axis] + step],
            device_id=shifted(axis, step),
            device_id_type=MESH,
        )

    def reduce_start(axis, value):
        reds[axis][me[axis]] = value
        for step in range(1, sizes[axis]):
            exchange(axis, step, me[axis]).start()

    def reduce_done(axis):
        for step in range(1, sizes[axis]):
            slot = lax.rem(me[axis] - step + sizes[axis], sizes[axis])
            exchange(axis, step, slot).wait_recv()
        total = reds[axis][0]
        for slot in range(1, sizes[axis]):
            total = total + reds[axis][slot]
        return total

    def setup_bonds(bx, by, bz, b):
        blocks, lanes, stiff = [], [], []
        for k in range(2):
            partner = part_ref[k, pl.ds(b, 1), :]
            blocks.append(jnp.broadcast_to(partner // BLK, (4, BLK)))
            lanes.append(jnp.broadcast_to(partner % BLK, (4, BLK)))
            stiff.append(jnp.where(coord, stiff_ref[k, pl.ds(b, 1), :], 0.0))
        block = jnp.concatenate(blocks, 0)
        lane_s[b] = jnp.concatenate(lanes, 0)
        spring[b] = jnp.concatenate(stiff, 0)
        face = jnp.zeros((8, BLK), jnp.int32)
        for f in range(1, 7):
            m = FACES[f]
            place = ((bx + 1 + m[0]) * (SBY + 2) + by + 1 + m[1]) * (SBZ + 2) + bz + 1 + m[2]
            face = jnp.where(block == place, f, face)
        face_s[b] = face

    def bond(n, bx, by, bz, b):
        own = ext[n, bx + 1, by + 1, bz + 1]
        lanes = lane_s[b]
        face = face_s[b]
        got = None
        for f in range(7):
            m = FACES[f]
            source = own if f == 0 else ext[n, bx + 1 + m[0], by + 1 + m[1], bz + 1 + m[2]]
            twice = jnp.concatenate([source, source], 0)
            found = jnp.take_along_axis(twice, lanes, axis=1, mode="promise_in_bounds")
            if f == 0:
                got = found
            else:
                got = jnp.where(face == f, found + vec8(*(float(c) for c in m)), got)
        pull = spring[b] * (got - jnp.concatenate([own, own], 0))
        return own, pull[:4] + pull[4:]

    def prepare(n, ex, ey, ez, mine=None):
        block = ext[n, ex, ey, ez]
        off = vec4(
            jnp.asarray(ex - 1, f32), jnp.asarray(ey - 1, f32), jnp.asarray(ez - 1, f32)
        )
        x = block + off
        square = jnp.where(coord, x * x, 0.0)
        norm = jnp.sum(square, 0, keepdims=True)
        amount = block[3:4]
        first = jnp.where(row4 == 0, 1.0, 0.0)
        other = jnp.concatenate([jnp.where(coord, -2.0 * x, norm), first], 0)
        h, m, l = split3(other)
        e = (ex * (SBY + 2) + ey) * (SBZ + 2) + ez
        far_s[e] = jnp.concatenate([h, m, h, m, l, h], 0).astype(jnp.bfloat16)
        vh, vm, vl = split3(jnp.where(coord, x * amount, amount))
        val_s[e] = jnp.concatenate([vh, vm, vl, jnp.zeros((4, BLK), f32)], 0).astype(jnp.bfloat16)
        if mine is not None:
            own = jnp.concatenate(
                [jnp.where(coord, x, 1.0), jnp.where(row4 == 0, norm, 0.0)], 0
            )
            h, m, l = split3(own)
            stack = jnp.concatenate([h, h, m, m, h, l, jnp.zeros((80, BLK), f32)], 0)
            own_s[mine] = jnp.transpose(stack)[:, :48].astype(jnp.bfloat16)

    def prepare_ghosts(n):
        def side_x(i, carry):
            for ez in range(SBZ + 2):
                prepare(n, 0, i, ez)
                prepare(n, SBX + 1, i, ez)
            return carry

        lax.fori_loop(0, SBY + 2, side_x, 0)

        def side_yz(i, carry):
            for ez in range(SBZ + 2):
                prepare(n, i, 0, ez)
                prepare(n, i, SBY + 1, ez)
            for ey in range(1, SBY + 1):
                prepare(n, i, ey, 0)
                prepare(n, i, ey, SBZ + 1)
            return carry

        lax.fori_loop(1, SBX + 1, side_yz, 0)

    scale = -math.log2(math.e) / (2.0 * gauss_width * gauss_width)

    def pair(n, bx, by, bz, b):
        own = own_s[b]
        acc = jnp.zeros((BLK, 16), f32)
        for j in range(0, list_ref.shape[1], 2):
            p, q = list_ref[b, j], list_ref[b, j + 1]
            far = jnp.concatenate([far_s[p], far_s[q]], 1)
            val = jnp.concatenate([val_s[p], val_s[q]], 1)
            distance = lax.dot_general(
                own, far, (((1,), (0,)), ((), ())), preferred_element_type=f32
            )
            taper = jnp.maximum(1.0 - distance * (1.0 / (cutoff_radius * cutoff_radius)), 0.0)
            weight = jnp.exp2(distance * scale) * (taper * taper)
            high = weight.astype(jnp.bfloat16)
            low = (weight - high.astype(f32)).astype(jnp.bfloat16)
            for part in (high, low):
                acc = acc + lax.dot_general(
                    part, val, (((1,), (1,)), ((), ())), preferred_element_type=f32
                )
        sums = jnp.transpose(acc)
        sums = sums[0:4] + sums[4:8] + sums[8:12]
        block = ext[n, bx + 1, by + 1, bz + 1]
        x = block + vec4(jnp.asarray(bx, f32), jnp.asarray(by, f32), jnp.asarray(bz, f32))
        force = block[3:4] * (x * sums[3:4] - sums)
        return jnp.where(coord, (pair_scale / (gauss_width * gauss_width)) * force, 0.0)

    def start_halo(n):
        for k in range(26 if n % 2 else 6):
            halo(n, k).start()

    def wait_halo(n, lo, hi):
        for k in range(lo, hi):
            halo(n, k).wait_recv()

    def bond_step(n, kick, drift):
        def body(bx, by, bz, b):
            own, force = bond(n, bx, by, bz, b)
            v = v_s[b] + kick * force
            v_s[b] = v
            if drift:
                ext[n + 1, bx + 1, by + 1, bz + 1] = own + inner_step * v

        spots(body)

    start_halo(0)
    spots(setup_bonds)
    wait_halo(0, 0, 6)
    bond_step(0, inner_step, True)

    start_halo(1)
    spots(lambda bx, by, bz, b: prepare(1, bx + 1, by + 1, bz + 1, b))
    wait_halo(1, 0, 26)
    bond_step(1, inner_step, False)
    prepare_ghosts(1)

    def middle(b, carry):
        bx, by, bz = b // (SBY * SBZ), b // SBZ % SBY, b % SBZ
        v = v_s[b] + (2.0 * inner_step) * pair(1, bx, by, bz, b)
        v_s[b] = v
        ext[2, bx + 1, by + 1, bz + 1] = ext[1, bx + 1, by + 1, bz + 1] + inner_step * v
        return carry

    lax.fori_loop(0, NB, middle, 0)

    start_halo(2)
    cell_ids = lax.broadcasted_iota(jnp.int32, (1, cells), 1)
    for b in range(NB):
        hot[b : b + 1, :] = jnp.where(cell_ids == cell_ref[0, 0, 0, b], 1.0, 0.0)
    wait_halo(2, 0, 6)
    bond_step(2, inner_step, True)

    start_halo(3)
    moments = jnp.zeros((4, cells), f32)
    for bx, by, bz in itertools.product(range(SBX), range(SBY), range(SBZ)):
        b = (bx * SBY + by) * SBZ + bz
        block = ext[3, bx + 1, by + 1, bz + 1]
        placed = jnp.where(
            coord,
            block
            + vec4(
                (me[0] * SBX + bx).astype(f32),
                (me[1] * SBY + by).astype(f32),
                (me[2] * SBZ + bz).astype(f32),
            ),
            1.0,
        )
        summed = jnp.sum(placed * charge_live[b : b + 1, :], 1, keepdims=True)
        moments = moments + summed * hot[b : b + 1, :]
        for c in range(3):
            pos_out[c, b : b + 1, :] = block[c : c + 1] + float((bx, by, bz)[c])
    reduce_start(0, moments)
    spots(lambda bx, by, bz, b: prepare(3, bx + 1, by + 1, bz + 1, b))
    wait_halo(3, 0, 26)
    bond_step(3, half_step, False)
    prepare_ghosts(3)

    def final(b, carry):
        bx, by, bz = b // (SBY * SBZ), b // SBZ % SBY, b % SBZ
        v_s[b] = v_s[b] + inner_step * pair(3, bx, by, bz, b)
        return carry

    quarter = NB // 4
    lax.fori_loop(0, quarter, final, 0)
    reduce_start(1, reduce_done(0))
    lax.fori_loop(quarter, 2 * quarter, final, 0)
    reduce_start(2, reduce_done(1))
    lax.fori_loop(2 * quarter, NB, final, 0)
    totals = reduce_done(2)

    one_hot = hot[...]
    charge_sum = totals[3:4]
    separation, dipole, centres = [], [], []
    for c in range(3):
        centre = frac_ref[c : c + 1, :] * float(sizes[c] * SIDES[c])
        target = jnp.sum(one_hot * centre, 1, keepdims=True)
        separation.append(target - centre)
        dipole.append(totals[c : c + 1] - charge_sum * centre)
    distance = sum(s * s for s in separation) + soften * soften
    inverse = lax.rsqrt(distance)
    cube = inverse * inverse * inverse
    fifth = cube * inverse * inverse
    dot = sum(d * s for d, s in zip(dipole, separation))
    along = charge_sum * cube + 3.0 * dot * fifth
    for b in range(NB):
        for c in range(3):
            vel_out[c, b : b + 1, :] = v_s[b, c : c + 1, :]
    for c in range(3):
        field = jnp.sum(along * separation[c] - dipole[c] * cube, 1, keepdims=True)
        vel_out[c] = vel_out[c] + outer_half * coulomb * (charge_live * field)

    for n in range(4):
        for k in range(26 if n % 2 else 6):
            halo(n, k).wait_send()
    for axis in range(3):
        for step in range(1, sizes[axis]):
            exchange(axis, step, me[axis]).wait_send()


def per_device(
    sizes,
    positions,
    velocities,
    strength,
    charge,
    bond_stiffness,
    bond_partner,
    pair_blocks,
    tile_count,
    block_cell,
    cell_frac,
    bond_force,
    pair_force,
    far_force,
):
    f32 = jnp.float32
    cells = cell_frac.shape[1]
    vmem = pl.BlockSpec(memory_space=pltpu.VMEM)
    smem = pl.BlockSpec(memory_space=pltpu.SMEM)
    wide = lambda x: x.reshape(x.shape[0], NB, BLK)
    flat = lambda x: x.reshape(NB, BLK)
    moved = sum(sizes)
    outs = pl.pallas_call(
        functools.partial(kernel, sizes),
        out_shape=[jax.ShapeDtypeStruct((3, NB, BLK), f32)] * 2,
        in_specs=[vmem] * 10 + [smem] * 3,
        out_specs=[vmem] * 2,
        scratch_shapes=[
            pltpu.VMEM((4, SBX + 2, SBY + 2, SBZ + 2, 4, BLK), f32),
            pltpu.VMEM((NB, 4, BLK), f32),
            pltpu.VMEM((NB, 8, BLK), f32),
            pltpu.VMEM((NB, 8, BLK), jnp.int32),
            pltpu.VMEM((NB, 8, BLK), jnp.int32),
            pltpu.VMEM((NB, BLK, 48), jnp.bfloat16),
            pltpu.VMEM(((SBX + 2) * (SBY + 2) * (SBZ + 2), 48, BLK), jnp.bfloat16),
            pltpu.VMEM(((SBX + 2) * (SBY + 2) * (SBZ + 2), 16, BLK), jnp.bfloat16),
            pltpu.VMEM((NB, cells), f32),
            pltpu.VMEM((sizes[0], 4, cells), f32),
            pltpu.VMEM((sizes[1], 4, cells), f32),
            pltpu.VMEM((sizes[2], 4, cells), f32),
            pltpu.SemaphoreType.DMA((4, 26)),
            pltpu.SemaphoreType.DMA((4, 26)),
            pltpu.SemaphoreType.DMA((moved,)),
            pltpu.SemaphoreType.DMA((moved,)),
        ],
        compiler_params=pltpu.CompilerParams(collective_id=0, has_side_effects=True),
    )(
        wide(positions),
        wide(velocities),
        flat(strength),
        flat(charge),
        wide(bond_stiffness),
        wide(bond_partner),
        cell_frac,
        wide(bond_force),
        wide(pair_force),
        wide(far_force),
        pair_blocks.reshape(pair_blocks.shape[3:]),
        tile_count,
        block_cell,
    )
    return outs[0].reshape(positions.shape), outs[1].reshape(velocities.shape)


def solution(mesh):
    sizes = tuple(mesh.shape[a] for a in AXES)
    in_specs = (
        P(None, "gx", "gy", "gz", None),
        P(None, "gx", "gy", "gz", None),
        P("gx", "gy", "gz", None),
        P("gx", "gy", "gz", None),
        P(None, "gx", "gy", "gz", None),
        P(None, "gx", "gy", "gz", None),
        P("gx", "gy", "gz", None, None),
        P("gx", "gy", "gz"),
        P("gx", "gy", "gz", None),
        P(),
        P(None, "gx", "gy", "gz", None),
        P(None, "gx", "gy", "gz", None),
        P(None, "gx", "gy", "gz", None),
    )
    out_specs = (P(None, "gx", "gy", "gz", None), P(None, "gx", "gy", "gz", None))
    return jax.shard_map(
        functools.partial(per_device, sizes),
        mesh=mesh,
        in_specs=in_specs,
        out_specs=out_specs,
        check_vma=False,
    )
```

profile of v0, /device:TPU:0, one launch (start us, length us, event | category | flops | bytes accessed | tf_op | source)
XLA Modules:
  0.0 84.1 jit_solution(5632038339070762249)
XLA Ops:
  1.3 0.0 copy-start.1
  1.3 0.7 copy-done.1
  2.0 0.7 copy.18
  2.6 79.4 %shard_map.140 = (f32[3,32,128]{2,1,0:T(8,128)}, f32[3,32,128]{2,1,0:T(8,128)}) custom-call(f32[3,32,128]{2,1,0:T(8,128)} %bitcast.15, f32[3,32,128]{2,1,0:T(8,128)} %bitcast.16, f32[32,128]{1,0:T(8,128)} %bitcast.22, f32[32,128]{1,0:T(8,128)} %bitcast.23, f32[2,32,128]{2,1,0:T(8,128)} %bitcast.20, s32[2,32,128]{2,1,0:T(8,128)} %bitcast.21, ...), custom_call_target="tpu_custom_call" | custom-call | tf_op jit(solution)/shard_map/pallas_call | solution.py:442
  82.1 0.0 copy-start
  82.1 1.4 %copy.24 = f32[3,1,1,1,4096]{4,3,2,1,0:T(1,128)} copy(f32[3,1,1,1,4096]{4,3,2,1,0:T(1,128)} %bitcast.14) | data formatting | bytes 98304
  83.5 0.0 copy-done
  83.5 0.6 copy.25
Async XLA Ops:
  1.3 0.7 copy-start.1
  82.1 1.4 %copy-start = (f32[3,32,128]{2,1,0:T(8,128)S(1)}, f32[3,32,128]{2,1,0:T(8,128)}, u32[]{:S(2)}) copy-start(f32[3,32,128]{2,1,0:T(8,128)} %get-tuple-element.5) | copy-start | bytes 147460
where the time goes:
time: 84.4 us; the launch traced here: 84.1 us
  Pallas kernels  79.4 us (94%)
  local copies, waits for them, and re-layouts  3.42 us (4%)
  between operations  1.3 us (2%)
    pallas_call x1, Pallas kernels, per_device(): pl.pallas_call(functools.partial(kernel, sizes), out_shape=[jax.ShapeDtyp...  79.4 us
    unnamed x7, local copies, waits for them, and re-layouts  3.42 us

commit v1 on v0

--- a/solution.py
+++ b/solution.py
@@ -44,8 +44,17 @@
     return high, middle, x - high - middle
 
 
-def kernel(
+def kernel(sizes, *refs):
+    fetched, sem = refs[-11:-1], refs[-1]
+    copies = [pltpu.make_async_copy(refs[i], fetched[i], sem.at[i]) for i in range(10)]
+    for copy in copies:
+        copy.start()
+    body(sizes, copies, *fetched, *refs[10:-11])
+
+
+def body(
     sizes,
+    copies,
     pos_ref,
     vel_ref,
     str_ref,
@@ -102,6 +111,9 @@
             pl.semaphore_signal(barrier, inc=1, device_id=shifted(axis, step), device_id_type=MESH)
             expected += 1
 
+    for copy in copies:
+        copy.wait()
+
     row4 = lax.broadcasted_iota(jnp.int32, (4, BLK), 0)
     row8 = lax.broadcasted_iota(jnp.int32, (8, BLK), 0)
 
@@ -281,22 +293,23 @@
 
     def pair(n, bx, by, bz, b):
         own = own_s[b]
-        acc = jnp.zeros((BLK, 16), f32)
-        for j in range(0, list_ref.shape[1], 2):
-            p, q = list_ref[b, j], list_ref[b, j + 1]
+        highs, lows, vals = [], [], []
+        for j in range(0, list_ref.shape[0], 2):
+            p, q = list_ref[j, b], list_ref[j + 1, b]
             far = jnp.concatenate([far_s[p], far_s[q]], 1)
-            val = jnp.concatenate([val_s[p], val_s[q]], 1)
+            vals.append(jnp.concatenate([val_s[p], val_s[q]], 1))
             distance = lax.dot_general(
                 own, far, (((1,), (0,)), ((), ())), preferred_element_type=f32
             )
             taper = jnp.maximum(1.0 - distance * (1.0 / (cutoff_radius * cutoff_radius)), 0.0)
             weight = jnp.exp2(distance * scale) * (taper * taper)
             high = weight.astype(jnp.bfloat16)
-            low = (weight - high.astype(f32)).astype(jnp.bfloat16)
-            for part in (high, low):
-                acc = acc + lax.dot_general(
-                    part, val, (((1,), (1,)), ((), ())), preferred_element_type=f32
-                )
+            highs.append(high)
+            lows.append((weight - high.astype(f32)).astype(jnp.bfloat16))
+        acc = lax.dot_general(
+            jnp.concatenate(highs + lows, 1), jnp.concatenate(vals + vals, 1),
+            (((1,), (1,)), ((), ())), preferred_element_type=f32,
+        )
         sums = jnp.transpose(acc)
         sums = sums[0:4] + sums[4:8] + sums[8:12]
         block = ext[n, bx + 1, by + 1, bz + 1]
@@ -329,8 +342,9 @@
 
     start_halo(1)
     spots(lambda bx, by, bz, b: prepare(1, bx + 1, by + 1, bz + 1, b))
-    wait_halo(1, 0, 26)
+    wait_halo(1, 0, 6)
     bond_step(1, inner_step, False)
+    wait_halo(1, 6, 26)
     prepare_ghosts(1)
 
     def middle(b, carry):
@@ -340,7 +354,7 @@
         ext[2, bx + 1, by + 1, bz + 1] = ext[1, bx + 1, by + 1, bz + 1] + inner_step * v
         return carry
 
-    lax.fori_loop(0, NB, middle, 0)
+    lax.fori_loop(0, NB, middle, 0, unroll=4)
 
     start_halo(2)
     cell_ids = lax.broadcasted_iota(jnp.int32, (1, cells), 1)
@@ -370,8 +384,9 @@
             pos_out[c, b : b + 1, :] = block[c : c + 1] + float((bx, by, bz)[c])
     reduce_start(0, moments)
     spots(lambda bx, by, bz, b: prepare(3, bx + 1, by + 1, bz + 1, b))
-    wait_halo(3, 0, 26)
+    wait_halo(3, 0, 6)
     bond_step(3, half_step, False)
+    wait_halo(3, 6, 26)
     prepare_ghosts(3)
 
     def final(b, carry):
@@ -380,11 +395,11 @@
         return carry
 
     quarter = NB // 4
-    lax.fori_loop(0, quarter, final, 0)
+    lax.fori_loop(0, quarter, final, 0, unroll=4)
     reduce_start(1, reduce_done(0))
-    lax.fori_loop(quarter, 2 * quarter, final, 0)
+    lax.fori_loop(quarter, 2 * quarter, final, 0, unroll=4)
     reduce_start(2, reduce_done(1))
-    lax.fori_loop(2 * quarter, NB, final, 0)
+    lax.fori_loop(2 * quarter, NB, final, 0, unroll=4)
     totals = reduce_done(2)
 
     one_hot = hot[...]
@@ -439,10 +454,22 @@
     wide = lambda x: x.reshape(x.shape[0], NB, BLK)
     flat = lambda x: x.reshape(NB, BLK)
     moved = sum(sizes)
+    operands = (
+        wide(positions),
+        wide(velocities),
+        flat(strength),
+        flat(charge),
+        wide(bond_stiffness),
+        wide(bond_partner),
+        cell_frac,
+        wide(bond_force),
+        wide(pair_force),
+        wide(far_force),
+    )
     outs = pl.pallas_call(
         functools.partial(kernel, sizes),
         out_shape=[jax.ShapeDtypeStruct((3, NB, BLK), f32)] * 2,
-        in_specs=[vmem] * 10 + [smem] * 3,
+        in_specs=[pl.BlockSpec(memory_space=pl.ANY)] * 10 + [smem] * 3,
         out_specs=[vmem] * 2,
         scratch_shapes=[
             pltpu.VMEM((4, SBX + 2, SBY + 2, SBZ + 2, 4, BLK), f32),
@@ -461,20 +488,13 @@
             pltpu.SemaphoreType.DMA((4, 26)),
             pltpu.SemaphoreType.DMA((moved,)),
             pltpu.SemaphoreType.DMA((moved,)),
+            *[pltpu.VMEM(x.shape, x.dtype) for x in operands],
+            pltpu.SemaphoreType.DMA((len(operands),)),
         ],
         compiler_params=pltpu.CompilerParams(collective_id=0, has_side_effects=True),
     )(
-        wide(positions),
-        wide(velocities),
-        flat(strength),
-        flat(charge),
-        wide(bond_stiffness),
-        wide(bond_partner),
-        cell_frac,
-        wide(bond_force),
-        wide(pair_force),
-        wide(far_force),
-        pair_blocks.reshape(pair_blocks.shape[3:]),
+        *operands,
+        jnp.swapaxes(pair_blocks.reshape(pair_blocks.shape[3:]), 0, 1),
         tile_count,
         block_cell,
     )

time: 84.4 us -> 55.9 us (0.66)
  Pallas kernels: 79.4 us -> 52.2 us
  local copies, waits for them, and re-layouts: 3.42 us -> 2.06 us
    pallas_call x1, Pallas kernels: 79.4 us -> 52.2 us  [per_device(): pl.pallas_call(functools.partial(kernel, sizes), out_shape=[jax.ShapeDtyp...]
    unnamed x7 -> x4, local copies, waits for them, and re-layouts: 3.42 us -> 2.06 us
where the time goes in v1:
time: 55.9 us; the launch traced here: 55.6 us
  Pallas kernels  52.2 us (93%)
  local copies, waits for them, and re-layouts  2.06 us (4%)
  between operations  1.3 us (2%)
    pallas_call x1, Pallas kernels, per_device(): pl.pallas_call(functools.partial(kernel, sizes), out_shape=[jax.ShapeDtyp...  52.2 us
    unnamed x4, local copies, waits for them, and re-layouts  2.06 us

profile of v1, /device:TPU:0, one launch (start us, length us, event | category | flops | bytes accessed | tf_op | source)
XLA Modules:
  0.0 55.6 jit_solution(12220461331288719748)
XLA Ops:
  1.3 52.2 %shard_map.140 = (f32[3,32,128]{2,1,0:T(8,128)}, f32[3,32,128]{2,1,0:T(8,128)}) custom-call(f32[3,32,128]{2,1,0:T(8,128)} %bitcast.16, f32[3,32,128]{2,1,0:T(8,128)} %bitcast.17, f32[32,128]{1,0:T(8,128)} %bitcast.23, f32[32,128]{1,0:T(8,128)} %bitcast.24, f32[2,32,128]{2,1,0:T(8,128)} %bitcast.21, s32[2,32,128]{2,1,0:T(8,128)} %bitcast.22, ...), custom_call_target="tpu_custom_call" | custom-call | tf_op jit(solution)/shard_map/pallas_call | solution.py:469
  53.5 0.0 copy-start
  53.5 1.4 %copy.22 = f32[3,1,1,1,4096]{4,3,2,1,0:T(1,128)} copy(f32[3,1,1,1,4096]{4,3,2,1,0:T(1,128)} %bitcast.15) | data formatting | bytes 98304
  55.0 0.0 copy-done
  55.0 0.6 %copy.23 = f32[3,1,1,1,4096]{4,3,2,1,0:T(1,128)} copy(f32[3,1,1,1,4096]{4,3,2,1,0:T(1,128)S(1)} %bitcast.14) | data formatting | bytes 98304
Async XLA Ops:
  53.5 1.4 %copy-start = (f32[3,32,128]{2,1,0:T(8,128)S(1)}, f32[3,32,128]{2,1,0:T(8,128)}, u32[]{:S(2)}) copy-start(f32[3,32,128]{2,1,0:T(8,128)} %get-tuple-element.5) | copy-start | bytes 147460
